TPU v7x, 32 devices: a whole 2x2x4 slice. The times are simulated.
32 devices in a mesh: row: 8 (over y, x, core), col: 4 (over z).
Axes of the slice: x: 2, y: 2, z: 4, core: 2. Of those that a mesh axis runs over, the one named last changes fastest.
Arguments:
- value_proj: float32 [8, 4, 1024, 512], P('row', 'col'), may hold values from -6 to 6
- token_pool: bfloat16 [8, 4, 1536, 1024], P('row', 'col'), may hold values from -6 to 6
- target_pool: bfloat16 [8, 4, 1536, 1024], P('row', 'col'), may hold values from -6 to 6
- batch_ids: int32 [8, 4, 3, 1536], P('row', 'col'), may hold values from 0 to 1535
- frozen_out: bfloat16 [512, 1024], replicated, may hold values from -0.25 to 0.25
- numerators: int32 [3], replicated, may hold values from 4 to 15
Outputs:
- final_proj: float32 [8, 4, 1024, 512], P('row', 'col')
- final_tracker: float32 [8, 4, 1024, 512], P('row', 'col')
All inputs are finite; a program needn't handle non-finite values.
Results may differ from a plain program's by a relative error of at most 0.017.
Values sent between devices are 32-bit elements; how exact they have to be, the bound alone decides.
A program may use at most 128 MiB of HBM per device.

v0:
```python
import functools
import math

import jax
import jax.numpy as jnp
from jax import lax
from jax.experimental import pallas as pl
from jax.experimental.pallas import tpu as pltpu
from jax.sharding import PartitionSpec as P

MESH = pl.DeviceIdType.MESH
step_rate = 0.2
PIECES = 8
AXES = ("row", "col")


def kernel(sizes, x0_ref, tok_hbm, tgt_hbm, ids_hbm, fo_hbm, num_hbm, outx_ref, outy_ref,
           tok, tgt, ids, fo, num_ref, x0, x1, g0, g1, g2, y1, xb, bp,
           x0_in, g0_in, x1_in, y1_in, local_sem, send_sem, recv_sem):
    pool, width = tok.shape
    features = x0.shape[1]
    factor = width ** (-0.5)
    f32, bf16 = jnp.float32, jnp.bfloat16
    piece = width // PIECES
    right, left = {}, {}
    for axis, n in zip(AXES, sizes):
        me = lax.axis_index(axis)
        right[axis], left[axis] = lax.rem(me + 1, n), lax.rem(me + n - 1, n)

    barrier = pltpu.get_barrier_semaphore()
    for axis in AXES:
        for there in (left, right):
            pl.semaphore_signal(
                barrier, inc=1, device_id={axis: there[axis]}, device_id_type=MESH
            )
    loads = []
    for slot, (source, target) in enumerate(
        (
            (x0_ref, x0), (tok_hbm, tok), (fo_hbm, fo),
            (tgt_hbm, tgt), (ids_hbm, ids), (num_hbm, num_ref),
        )
    ):
        load = pltpu.make_async_copy(source, target, local_sem.at[slot])
        load.start()
        loads.append(load)

    loads[0].wait()
    pl.semaphore_wait(barrier, 4)

    def send(source, target, which, slot):
        copy = pltpu.make_async_remote_copy(
            src_ref=source,
            dst_ref=target,
            send_sem=send_sem.at[which, slot],
            recv_sem=recv_sem.at[which, slot],
            device_id={AXES[which]: right[AXES[which]]},
            device_id_type=MESH,
        )
        copy.start()
        return copy

    def send_both(source, target, slot):
        return [send(source, target.at[which], which, slot) for which in (1, 0)]

    x0_copies = send_both(x0, x0_in, 0)

    step = math.gcd(width, 64)

    def by_rows(first, last, body):
        def go(i, carry):
            body(pl.ds(pl.multiple_of(i * step, step), step))
            return carry

        lax.fori_loop(first // step, last // step, go, 0)

    def mixed(own, arrived, rows):
        return w[0] * own[rows, :] + w[1] * arrived[0, rows, :] + w[2] * arrived[1, rows, :]

    block = math.gcd(pool, 256)
    wide = math.gcd(width, 256)

    def gradient(which, out):
        def forward(i, carry):
            rows = pl.ds(pl.multiple_of(i * block, block), block)
            preact = jnp.dot(tok[rows, :], xb[...], preferred_element_type=f32) * factor
            s = jax.nn.sigmoid(preact)
            hidden = (preact * s).astype(bf16)
            output = jnp.dot(hidden, fo[...], preferred_element_type=f32)
            error_term = (output - tgt[rows, :].astype(f32)).astype(bf16)
            back_hidden = lax.dot_general(
                error_term, fo[...], (((1,), (1,)), ((), ())), preferred_element_type=f32
            )
            slope = s * (1.0 + preact * (1.0 - s))
            row_ids = lax.broadcasted_iota(jnp.int32, (block, ids.shape[2]), 0) + i * block
            hits = jnp.where(row_ids == ids[which], 1.0, 0.0)
            times = jnp.sum(hits, axis=1, keepdims=True)
            bp[rows, :] = (back_hidden * slope * times).astype(bf16)
            return carry

        lax.fori_loop(0, pool // block, forward, 0)

        for j in range(width // wide):
            cols = pl.ds(j * wide, wide)
            out[cols, :] = (
                lax.dot_general(
                    tok[:, cols], bp[...], (((0,), (0,)), ((), ())), preferred_element_type=f32
                )
                * factor
            )

    for load in loads[1:]:
        load.wait()

    counts = [jnp.full((8, 128), num_ref[i], jnp.int32).astype(f32) for i in range(3)]
    total = counts[0] + counts[1] + counts[2]
    w = [(c / total)[0:1, 0:1] for c in counts]

    def first_round(rows):
        xb[rows, :] = x0[rows, :].astype(bf16)

    by_rows(0, width, first_round)
    gradient(0, g0)
    g0_copies = send_both(g0, g0_in, 1)

    for copy in x0_copies:
        copy.wait()

    def first_move(rows):
        moved = mixed(x0, x0_in, rows) - step_rate * g0[rows, :]
        x1[rows, :] = moved
        xb[rows, :] = moved.astype(bf16)

    by_rows(0, width, first_move)
    x1_copies = send_both(x1, x1_in, 2)
    gradient(1, g1)
    for copy in g0_copies:
        copy.wait()

    def first_track(rows):
        y1[rows, :] = mixed(g0, g0_in, rows) + g1[rows, :] - g0[rows, :]

    by_rows(0, width, first_track)
    y1_copies = []
    for part in range(PIECES):
        rows = pl.ds(part * piece, piece)
        y1_copies.append(
            [send(y1.at[rows], y1_in.at[which, rows], which, 3 + part) for which in (1, 0)]
        )

    for copy in x1_copies:
        copy.wait()

    def second_move(rows):
        moved = mixed(x1, x1_in, rows) - step_rate * y1[rows, :]
        outx_ref[rows, :] = moved
        xb[rows, :] = moved.astype(bf16)

    by_rows(0, width, second_move)
    gradient(2, g2)

    def second_track(rows):
        outy_ref[rows, :] = mixed(y1, y1_in, rows) + g2[rows, :] - g1[rows, :]

    for part in range(PIECES):
        for copy in y1_copies[part]:
            copy.wait()
        by_rows(part * piece, (part + 1) * piece, second_track)


def solution(mesh):
    sizes = tuple(mesh.shape[axis] for axis in AXES)

    def on_device(value_proj, token_pool, target_pool, batch_ids, frozen_out, numerators):
        width, features = value_proj.shape[2:]
        pool = token_pool.shape[2]
        rounds, batch = batch_ids.shape[2:]
        field = pltpu.VMEM((width, features), jnp.float32)
        arrivals = pltpu.VMEM((2, width, features), jnp.float32)
        in_hbm = pl.BlockSpec(memory_space=pltpu.HBM)
        shape = jax.ShapeDtypeStruct((width, features), jnp.float32)
        final_proj, final_tracker = pl.pallas_call(
            functools.partial(kernel, sizes),
            out_shape=(shape, shape),
            in_specs=[in_hbm] * 6,
            out_specs=(pl.BlockSpec(memory_space=pltpu.VMEM),) * 2,
            scratch_shapes=[
                pltpu.VMEM((pool, width), jnp.bfloat16),
                pltpu.VMEM((pool, width), jnp.bfloat16),
                pltpu.VMEM((rounds, 1, batch), jnp.int32),
                pltpu.VMEM((features, width), jnp.bfloat16),
                pltpu.SMEM(numerators.shape, jnp.int32),
                field, field, field, field, field, field,
                pltpu.VMEM((width, features), jnp.bfloat16),
                pltpu.VMEM((pool, features), jnp.bfloat16),
                arrivals, arrivals, arrivals, arrivals,
                pltpu.SemaphoreType.DMA((6,)),
                pltpu.SemaphoreType.DMA((2, 3 + PIECES)),
                pltpu.SemaphoreType.DMA((2, 3 + PIECES)),
            ],
            compiler_params=pltpu.CompilerParams(
                collective_id=0, has_side_effects=True, vmem_limit_bytes=48 * 2**20
            ),
        )(
            value_proj.reshape(width, features),
            token_pool.reshape(pool, width),
            target_pool.reshape(pool, width),
            batch_ids.reshape(rounds, 1, batch),
            frozen_out,
            numerators,
        )
        return final_proj[None, None], final_tracker[None, None]

    return jax.shard_map(
        on_device,
        mesh=mesh,
        in_specs=(
            P("row", "col", None, None),
            P("row", "col", None, None),
            P("row", "col", None, None),
            P("row", "col", None, None),
            P(),
            P(),
        ),
        out_specs=(P("row", "col", None, None), P("row", "col", None, None)),
        check_vma=False,
    )
```

profile of v0, /device:TPU:0, one launch (start us, length us, event | category | flops | bytes accessed | tf_op | source)
XLA Modules:
  0.0 193.7 jit_solution(8450544393574411212)
XLA Ops:
  0.6 0.0 copy-start
  0.6 1.2 copy-done
  1.9 0.0 copy-start.1
  1.9 0.7 copy-done.1
  2.6 0.0 copy-start.2
  2.6 0.7 copy-done.2
  3.2 187.8 %shard_map.77 = (f32[1024,512]{1,0:T(8,128)S(1)}, f32[1024,512]{1,0:T(8,128)S(1)}) custom-call(f32[1024,512]{1,0:T(8,128)} %bitcast.11, bf16[1536,1024]{1,0:T(8,128)(2,1)} %bitcast.9, bf16[1536,1024]{1,0:T(8,128)(2,1)} %bitcast.10, s32[3,1,1536]{2,1,0:T(1,128)S(1)} %bitcast.8, bf16[512,1024]{1,0:T(8,128)(2,1)S(1)} %copy-done, s32[3]{0:T(128)S(1)} %copy-done.2), custom_call_target="tpu_custom_call" | custom-call | tf_op jit(solution)/shard_map/pallas_call | solution.py:181
  191.1 1.3 copy.10
  192.4 1.3 copy.11
Async XLA Ops:
  0.6 1.2 copy-start
  1.9 0.7 copy-start.1
  2.6 0.7 copy-start.2
where the time goes:
time: 194 us
  Pallas kernels  188 us (97%)
  local copies, waits for them, and re-layouts  5.23 us (3%)
    pallas_call x1, Pallas kernels, on_device(): pl.pallas_call(functools.partial(kernel, sizes), out_shape=(shape, shape)...  188 us
    unnamed x8, local copies, waits for them, and re-layouts  5.23 us

commit v1 on v0

--- a/solution.py
+++ b/solution.py
@@ -44,7 +44,6 @@
         load.start()
         loads.append(load)
 
-    loads[0].wait()
     pl.semaphore_wait(barrier, 4)
 
     def send(source, target, which, slot):
@@ -62,7 +61,7 @@
     def send_both(source, target, slot):
         return [send(source, target.at[which], which, slot) for which in (1, 0)]
 
-    x0_copies = send_both(x0, x0_in, 0)
+    x0_copies = send_both(x0_ref, x0_in, 0)
 
     step = math.gcd(width, 64)
 
@@ -108,7 +107,7 @@
                 * factor
             )
 
-    for load in loads[1:]:
+    for load in loads:
         load.wait()
 
     counts = [jnp.full((8, 128), num_ref[i], jnp.int32).astype(f32) for i in range(3)]
@@ -165,6 +164,16 @@
         for copy in y1_copies[part]:
             copy.wait()
         by_rows(part * piece, (part + 1) * piece, second_track)
+
+
+def write_out(x_ref, y_ref, x_hbm, y_hbm, sems):
+    copies = []
+    for slot, (source, target) in enumerate(((x_ref, x_hbm), (y_ref, y_hbm))):
+        copy = pltpu.make_async_copy(source, target, sems.at[slot])
+        copy.start()
+        copies.append(copy)
+    for copy in copies:
+        copy.wait()
 
 
 def solution(mesh):
@@ -180,7 +189,7 @@
         shape = jax.ShapeDtypeStruct((width, features), jnp.float32)
         final_proj, final_tracker = pl.pallas_call(
             functools.partial(kernel, sizes),
-            out_shape=(shape, shape),
+            out_shape=(pltpu.VMEM((width, features), jnp.float32),) * 2,
             in_specs=[in_hbm] * 6,
             out_specs=(pl.BlockSpec(memory_space=pltpu.VMEM),) * 2,
             scratch_shapes=[
@@ -198,7 +207,7 @@
                 pltpu.SemaphoreType.DMA((2, 3 + PIECES)),
             ],
             compiler_params=pltpu.CompilerParams(
-                collective_id=0, has_side_effects=True, vmem_limit_bytes=48 * 2**20
+                collective_id=0, has_side_effects=True, vmem_limit_bytes=54_000_000
             ),
         )(
             value_proj.reshape(width, features),
@@ -208,6 +217,14 @@
             frozen_out,
             numerators,
         )
+        final_proj, final_tracker = pl.pallas_call(
+            write_out,
+            out_shape=(shape, shape),
+            in_specs=[pl.BlockSpec(memory_space=pltpu.VMEM)] * 2,
+            out_specs=(in_hbm,) * 2,
+            scratch_shapes=[pltpu.SemaphoreType.DMA((2,))],
+            compiler_params=pltpu.CompilerParams(vmem_limit_bytes=2**20),
+        )(final_proj, final_tracker)
         return final_proj[None, None], final_tracker[None, None]
 
     return jax.shard_map(

time: 194 us -> 191 us (0.985)
  local copies, waits for them, and re-layouts: 5.23 us -> 0 us
  Pallas kernels: 188 us -> 190 us
    unnamed x8 -> x0, local copies, waits for them, and re-layouts: 5.23 us -> none
    pallas_call x1 -> x2, Pallas kernels: 188 us -> 190 us  [the longest x1 188 us: on_device(): pl.pallas_call(functools.partial(kernel, sizes), out_shape=(pltpu.VMEM((w...]
where the time goes in v1:
time: 191 us
  Pallas kernels  190 us (99%)
    pallas_call x1, Pallas kernels, on_device(): pl.pallas_call(functools.partial(kernel, sizes), out_shape=(pltpu.VMEM((w...  188 us

profile of v1, /device:TPU:0, one launch (start us, length us, event | category | flops | bytes accessed | tf_op | source)
XLA Modules:
  0.0 190.7 jit_solution(10805345888092434162)
XLA Ops:
  0.6 188.1 %shard_map.77 = (f32[1024,512]{1,0:T(8,128)S(1)}, f32[1024,512]{1,0:T(8,128)S(1)}) custom-call(f32[1024,512]{1,0:T(8,128)} %bitcast.8, bf16[1536,1024]{1,0:T(8,128)(2,1)} %bitcast.6, bf16[1536,1024]{1,0:T(8,128)(2,1)} %bitcast.7, s32[3,1,1536]{2,1,0:T(1,128)} %bitcast.9, bf16[512,1024]{1,0:T(8,128)(2,1)} %fo_hbm.1, s32[3]{0:T(128)} %num_hbm.1), custom_call_target="tpu_custom_call" | custom-call | tf_op jit(solution)/shard_map/pallas_call | solution.py:190
  188.7 2.0 %shard_map.78 = (f32[1024,512]{1,0:T(8,128)}, f32[1024,512]{1,0:T(8,128)}) custom-call(f32[1024,512]{1,0:T(8,128)S(1)} %get-tuple-element.6.x_ref, f32[1024,512]{1,0:T(8,128)S(1)} %get-tuple-element.7.y_ref), custom_call_target="tpu_custom_call" | custom-call | tf_op jit(solution)/shard_map/pallas_call | solution.py:220

commit v2 on v1

--- a/solution.py
+++ b/solution.py
@@ -11,6 +11,7 @@
 MESH = pl.DeviceIdType.MESH
 step_rate = 0.2
 PIECES = 8
+OUT_PIECES = 4
 AXES = ("row", "col")
 
 
@@ -29,22 +30,10 @@
 
     barrier = pltpu.get_barrier_semaphore()
     for axis in AXES:
-        for there in (left, right):
-            pl.semaphore_signal(
-                barrier, inc=1, device_id={axis: there[axis]}, device_id_type=MESH
-            )
-    loads = []
-    for slot, (source, target) in enumerate(
-        (
-            (x0_ref, x0), (tok_hbm, tok), (fo_hbm, fo),
-            (tgt_hbm, tgt), (ids_hbm, ids), (num_hbm, num_ref),
-        )
-    ):
-        load = pltpu.make_async_copy(source, target, local_sem.at[slot])
-        load.start()
-        loads.append(load)
-
-    pl.semaphore_wait(barrier, 4)
+        pl.semaphore_signal(
+            barrier, inc=1, device_id={axis: left[axis]}, device_id_type=MESH
+        )
+    pl.semaphore_wait(barrier, len(AXES))
 
     def send(source, target, which, slot):
         copy = pltpu.make_async_remote_copy(
@@ -62,6 +51,17 @@
         return [send(source, target.at[which], which, slot) for which in (1, 0)]
 
     x0_copies = send_both(x0_ref, x0_in, 0)
+
+    loads = []
+    for slot, (source, target) in enumerate(
+        (
+            (x0_ref, x0), (tok_hbm, tok), (fo_hbm, fo),
+            (tgt_hbm, tgt), (ids_hbm, ids), (num_hbm, num_ref),
+        )
+    ):
+        load = pltpu.make_async_copy(source, target, local_sem.at[slot])
+        load.start()
+        loads.append(load)
 
     step = math.gcd(width, 64)
 
@@ -167,11 +167,14 @@
 
 
 def write_out(x_ref, y_ref, x_hbm, y_hbm, sems):
+    rows = x_ref.shape[0] // OUT_PIECES
     copies = []
-    for slot, (source, target) in enumerate(((x_ref, x_hbm), (y_ref, y_hbm))):
-        copy = pltpu.make_async_copy(source, target, sems.at[slot])
-        copy.start()
-        copies.append(copy)
+    for part in range(OUT_PIECES):
+        here = pl.ds(part * rows, rows)
+        for which, (source, target) in enumerate(((x_ref, x_hbm), (y_ref, y_hbm))):
+            copy = pltpu.make_async_copy(source.at[here], target.at[here], sems.at[which, part])
+            copy.start()
+            copies.append(copy)
     for copy in copies:
         copy.wait()
 
@@ -222,7 +225,7 @@
             out_shape=(shape, shape),
             in_specs=[pl.BlockSpec(memory_space=pltpu.VMEM)] * 2,
             out_specs=(in_hbm,) * 2,
-            scratch_shapes=[pltpu.SemaphoreType.DMA((2,))],
+            scratch_shapes=[pltpu.SemaphoreType.DMA((2, OUT_PIECES))],
             compiler_params=pltpu.CompilerParams(vmem_limit_bytes=2**20),
         )(final_proj, final_tracker)
         return final_proj[None, None], final_tracker[None, None]

time: 191 us -> 189 us (0.990)
  Pallas kernels: 190 us -> 188 us
where the time goes in v2:
time: 189 us
  Pallas kernels  188 us (99%)
    pallas_call x1, Pallas kernels, on_device(): pl.pallas_call(functools.partial(kernel, sizes), out_shape=(pltpu.VMEM((w...  186 us

profile of v2, /device:TPU:0, one launch (start us, length us, event | category | flops | bytes accessed | tf_op | source)
XLA Modules:
  0.0 189.0 jit_solution(5335510611216222446)
XLA Ops:
  0.6 186.3 %shard_map.77 = (f32[1024,512]{1,0:T(8,128)S(1)}, f32[1024,512]{1,0:T(8,128)S(1)}) custom-call(f32[1024,512]{1,0:T(8,128)} %bitcast.8, bf16[1536,1024]{1,0:T(8,128)(2,1)} %bitcast.6, bf16[1536,1024]{1,0:T(8,128)(2,1)} %bitcast.7, s32[3,1,1536]{2,1,0:T(1,128)} %bitcast.9, bf16[512,1024]{1,0:T(8,128)(2,1)} %fo_hbm.1, s32[3]{0:T(128)} %num_hbm.1), custom_call_target="tpu_custom_call" | custom-call | tf_op jit(solution)/shard_map/pallas_call | solution.py:193
  186.9 2.1 %shard_map.78 = (f32[1024,512]{1,0:T(8,128)}, f32[1024,512]{1,0:T(8,128)}) custom-call(f32[1024,512]{1,0:T(8,128)S(1)} %get-tuple-element.6.x_ref, f32[1024,512]{1,0:T(8,128)S(1)} %get-tuple-element.7.y_ref), custom_call_target="tpu_custom_call" | custom-call | tf_op jit(solution)/shard_map/pallas_call | solution.py:223

commit v3 on v1

--- a/solution.py
+++ b/solution.py
@@ -10,58 +10,107 @@
 
 MESH = pl.DeviceIdType.MESH
 step_rate = 0.2
-PIECES = 8
+HEAD = 64
 AXES = ("row", "col")
 
 
 def kernel(sizes, x0_ref, tok_hbm, tgt_hbm, ids_hbm, fo_hbm, num_hbm, outx_ref, outy_ref,
            tok, tgt, ids, fo, num_ref, x0, x1, g0, g1, g2, y1, xb, bp,
-           x0_in, g0_in, x1_in, y1_in, local_sem, send_sem, recv_sem):
+           x0_in, g0_in, x1_in, y1_in, far_in, relay_in,
+           local_sem, send_sem, recv_sem, extra_send, extra_recv, ready):
     pool, width = tok.shape
     features = x0.shape[1]
     factor = width ** (-0.5)
     f32, bf16 = jnp.float32, jnp.bfloat16
-    piece = width // PIECES
     right, left = {}, {}
     for axis, n in zip(AXES, sizes):
         me = lax.axis_index(axis)
         right[axis], left[axis] = lax.rem(me + 1, n), lax.rem(me + n - 1, n)
+    n_col = sizes[1]
+    col = lax.axis_index("col")
+    first, last, before = col == 0, col == n_col - 1, col == n_col - 2
+    size = min(HEAD, width // 2)
+    head, rest = pl.ds(0, size), pl.ds(size, width - size)
+    bulk, tail = pl.ds(0, width - size), pl.ds(width - size, size)
+
+    load_head = pltpu.make_async_copy(x0_ref.at[head], x0.at[head], local_sem.at[0])
+    load_head.start()
 
     barrier = pltpu.get_barrier_semaphore()
-    for axis in AXES:
-        for there in (left, right):
-            pl.semaphore_signal(
-                barrier, inc=1, device_id={axis: there[axis]}, device_id_type=MESH
-            )
+
+    def greet(axis, there):
+        pl.semaphore_signal(barrier, inc=1, device_id={axis: there}, device_id_type=MESH)
+
+    @pl.when(first)
+    def _():
+        greet("col", n_col - 2)
+
+    @pl.when(jnp.logical_not(last))
+    def _():
+        greet("col", left["col"])
+
+    @pl.when(before)
+    def _():
+        greet("col", n_col - 1)
+
+    greet("row", left["row"])
+
+    def copy_to(source, target, sends, recvs, device):
+        return pltpu.make_async_remote_copy(
+            src_ref=source, dst_ref=target, send_sem=sends, recv_sem=recvs,
+            device_id=device, device_id_type=MESH,
+        )
+
+    def describe(source, target, which, slot):
+        return copy_to(
+            source, target, send_sem.at[which, slot], recv_sem.at[which, slot],
+            {AXES[which]: right[AXES[which]]},
+        )
+
+    def describe_both(source, target, slot, rows):
+        return [
+            describe(source.at[rows], target.at[which, rows], which, slot) for which in (1, 0)
+        ]
+
+    far_copy = copy_to(
+        x0.at[head], far_in, extra_send.at[0], extra_recv.at[0], {"col": 0}
+    )
+    relay_copy = copy_to(
+        x0_in.at[1, head], relay_in, extra_send.at[1], extra_recv.at[1], {"row": right["row"]}
+    )
+
+    @pl.when(jnp.logical_not(last))
+    def _():
+        pl.semaphore_wait(barrier, 2)
+
+    @pl.when(last)
+    def _():
+        pl.semaphore_wait(barrier, 3)
+        pl.semaphore_signal(
+            ready, inc=1, device_id={"col": n_col - 2}, device_id_type=MESH
+        )
+
+    load_head.wait()
+
+    @pl.when(before)
+    def _():
+        far_copy.start()
+        pl.semaphore_wait(ready, 1)
+
+    x0_copies = describe_both(x0, x0_in, 0, head) + describe_both(x0_ref, x0_in, 1, rest)
+    for copy in x0_copies:
+        copy.start()
+
     loads = []
     for slot, (source, target) in enumerate(
         (
-            (x0_ref, x0), (tok_hbm, tok), (fo_hbm, fo),
+            (x0_ref.at[rest], x0.at[rest]), (tok_hbm, tok), (fo_hbm, fo),
             (tgt_hbm, tgt), (ids_hbm, ids), (num_hbm, num_ref),
         )
     ):
-        load = pltpu.make_async_copy(source, target, local_sem.at[slot])
+        load = pltpu.make_async_copy(source, target, local_sem.at[slot + 1])
         load.start()
         loads.append(load)
-
-    pl.semaphore_wait(barrier, 4)
-
-    def send(source, target, which, slot):
-        copy = pltpu.make_async_remote_copy(
-            src_ref=source,
-            dst_ref=target,
-            send_sem=send_sem.at[which, slot],
-            recv_sem=recv_sem.at[which, slot],
-            device_id={AXES[which]: right[AXES[which]]},
-            device_id_type=MESH,
-        )
-        copy.start()
-        return copy
-
-    def send_both(source, target, slot):
-        return [send(source, target.at[which], which, slot) for which in (1, 0)]
-
-    x0_copies = send_both(x0_ref, x0_in, 0)
 
     step = math.gcd(width, 64)
 
@@ -119,10 +168,16 @@
 
     by_rows(0, width, first_round)
     gradient(0, g0)
-    g0_copies = send_both(g0, g0_in, 1)
+    g0_copies = describe_both(g0, g0_in, 2, pl.ds(0, width))
+    for copy in g0_copies:
+        copy.start()
 
     for copy in x0_copies:
         copy.wait()
+
+    @pl.when(first)
+    def _():
+        relay_copy.start()
 
     def first_move(rows):
         moved = mixed(x0, x0_in, rows) - step_rate * g0[rows, :]
@@ -130,7 +185,15 @@
         xb[rows, :] = moved.astype(bf16)
 
     by_rows(0, width, first_move)
-    x1_copies = send_both(x1, x1_in, 2)
+    x1_head, x1_head_row = describe_both(x1, x1_in, 3, head)
+    x1_copies = [x1_head_row] + describe_both(x1, x1_in, 4, rest)
+
+    @pl.when(jnp.logical_not(last))
+    def _():
+        x1_head.start()
+
+    for copy in x1_copies:
+        copy.start()
     gradient(1, g1)
     for copy in g0_copies:
         copy.wait()
@@ -139,15 +202,40 @@
         y1[rows, :] = mixed(g0, g0_in, rows) + g1[rows, :] - g0[rows, :]
 
     by_rows(0, width, first_track)
-    y1_copies = []
-    for part in range(PIECES):
-        rows = pl.ds(part * piece, piece)
-        y1_copies.append(
-            [send(y1.at[rows], y1_in.at[which, rows], which, 3 + part) for which in (1, 0)]
-        )
+    y1_bulk = describe_both(y1, y1_in, 5, bulk)
+    y1_tail = describe_both(y1, y1_in, 6, tail)
+    for copy in y1_bulk + y1_tail:
+        copy.start()
 
     for copy in x1_copies:
         copy.wait()
+
+    @pl.when(jnp.logical_not(last))
+    def _():
+        x1_head.wait_send()
+
+    @pl.when(jnp.logical_not(first))
+    def _():
+        x1_head.wait_recv()
+
+    @pl.when(before)
+    def _():
+        far_copy.wait_send()
+
+    @pl.when(first)
+    def _():
+        relay_copy.wait()
+        far_copy.wait_recv()
+
+        def neighbour_move(rows):
+            x1_in[1, rows, :] = (
+                w[0] * x0_in[1, rows, :]
+                + w[1] * relay_in[rows, :]
+                + w[2] * far_in[rows, :]
+                - step_rate * g0_in[1, rows, :]
+            )
+
+        by_rows(0, size, neighbour_move)
 
     def second_move(rows):
         moved = mixed(x1, x1_in, rows) - step_rate * y1[rows, :]
@@ -160,10 +248,12 @@
     def second_track(rows):
         outy_ref[rows, :] = mixed(y1, y1_in, rows) + g2[rows, :] - g1[rows, :]
 
-    for part in range(PIECES):
-        for copy in y1_copies[part]:
-            copy.wait()
-        by_rows(part * piece, (part + 1) * piece, second_track)
+    for copy in y1_bulk:
+        copy.wait()
+    by_rows(0, width - size, second_track)
+    for copy in y1_tail:
+        copy.wait()
+    by_rows(width - size, width, second_track)
 
 
 def write_out(x_ref, y_ref, x_hbm, y_hbm, sems):
@@ -202,9 +292,14 @@
                 pltpu.VMEM((width, features), jnp.bfloat16),
                 pltpu.VMEM((pool, features), jnp.bfloat16),
                 arrivals, arrivals, arrivals, arrivals,
-                pltpu.SemaphoreType.DMA((6,)),
-                pltpu.SemaphoreType.DMA((2, 3 + PIECES)),
-                pltpu.SemaphoreType.DMA((2, 3 + PIECES)),
+                pltpu.VMEM((min(HEAD, width // 2), features), jnp.float32),
+                pltpu.VMEM((min(HEAD, width // 2), features), jnp.float32),
+                pltpu.SemaphoreType.DMA((7,)),
+                pltpu.SemaphoreType.DMA((2, 7)),
+                pltpu.SemaphoreType.DMA((2, 7)),
+                pltpu.SemaphoreType.DMA((2,)),
+                pltpu.SemaphoreType.DMA((2,)),
+                pltpu.SemaphoreType.REGULAR,
             ],
             compiler_params=pltpu.CompilerParams(
                 collective_id=0, has_side_effects=True, vmem_limit_bytes=54_000_000

time: 191 us -> 200 us (1.047)
  Pallas kernels: 190 us -> 199 us
    pallas_call x1, Pallas kernels: 188 us -> 197 us  [on_device(): pl.pallas_call(functools.partial(kernel, sizes), out_shape=(pltpu.VMEM((w...]
where the time goes in v3:
time: 200 us; the launch traced here: 199 us
  Pallas kernels  199 us (100%)
    pallas_call x1, Pallas kernels, on_device(): pl.pallas_call(functools.partial(kernel, sizes), out_shape=(pltpu.VMEM((w...  197 us

profile of v3, /device:TPU:0, one launch (start us, length us, event | category | flops | bytes accessed | tf_op | source)
XLA Modules:
  0.0 199.4 jit_solution(4719061703357704833)
XLA Ops:
  0.6 196.7 %shard_map.77 = (f32[1024,512]{1,0:T(8,128)S(1)}, f32[1024,512]{1,0:T(8,128)S(1)}) custom-call(f32[1024,512]{1,0:T(8,128)} %bitcast.8, bf16[1536,1024]{1,0:T(8,128)(2,1)} %bitcast.6, bf16[1536,1024]{1,0:T(8,128)(2,1)} %bitcast.7, s32[3,1,1536]{2,1,0:T(1,128)} %bitcast.9, bf16[512,1024]{1,0:T(8,128)(2,1)} %fo_hbm.1, s32[3]{0:T(128)} %num_hbm.1), custom_call_target="tpu_custom_call" | custom-call | tf_op jit(solution)/shard_map/pallas_call | solution.py:280
  197.3 2.0 %shard_map.78 = (f32[1024,512]{1,0:T(8,128)}, f32[1024,512]{1,0:T(8,128)}) custom-call(f32[1024,512]{1,0:T(8,128)S(1)} %get-tuple-element.6.x_ref, f32[1024,512]{1,0:T(8,128)S(1)} %get-tuple-element.7.y_ref), custom_call_target="tpu_custom_call" | custom-call | tf_op jit(solution)/shard_map/pallas_call | solution.py:315

commit v4 on v2

--- a/solution.py
+++ b/solution.py
@@ -11,13 +11,14 @@
 MESH = pl.DeviceIdType.MESH
 step_rate = 0.2
 PIECES = 8
-OUT_PIECES = 4
+EARLY = 3
 AXES = ("row", "col")
 
 
 def kernel(sizes, x0_ref, tok_hbm, tgt_hbm, ids_hbm, fo_hbm, num_hbm, outx_ref, outy_ref,
            tok, tgt, ids, fo, num_ref, x0, x1, g0, g1, g2, y1, xb, bp,
-           x0_in, g0_in, x1_in, y1_in, local_sem, send_sem, recv_sem):
+           x0_in, g0_in, x1_in, y1_in, far_in, mix2, mix3,
+           local_sem, send_sem, recv_sem, far_send, far_recv):
     pool, width = tok.shape
     features = x0.shape[1]
     factor = width ** (-0.5)
@@ -28,15 +29,37 @@
         me = lax.axis_index(axis)
         right[axis], left[axis] = lax.rem(me + 1, n), lax.rem(me + n - 1, n)
 
+    n_col = sizes[1]
+    col = lax.axis_index("col")
+    first, second, last = col == 0, col == 1, col == n_col - 1
+
+    def where(condition):
+        return pl.when(condition), pl.when(jnp.logical_not(condition))
+
     barrier = pltpu.get_barrier_semaphore()
     for axis in AXES:
         pl.semaphore_signal(
             barrier, inc=1, device_id={axis: left[axis]}, device_id_type=MESH
         )
-    pl.semaphore_wait(barrier, len(AXES))
-
-    def send(source, target, which, slot):
-        copy = pltpu.make_async_remote_copy(
+
+    @pl.when(second)
+    def _():
+        pl.semaphore_signal(
+            barrier, inc=1, device_id={"col": n_col - 1}, device_id_type=MESH
+        )
+
+    on_last, elsewhere = where(last)
+
+    @on_last
+    def _():
+        pl.semaphore_wait(barrier, 3)
+
+    @elsewhere
+    def _():
+        pl.semaphore_wait(barrier, 2)
+
+    def describe(source, target, which, slot):
+        return pltpu.make_async_remote_copy(
             src_ref=source,
             dst_ref=target,
             send_sem=send_sem.at[which, slot],
@@ -44,13 +67,26 @@
             device_id={AXES[which]: right[AXES[which]]},
             device_id_type=MESH,
         )
-        copy.start()
-        return copy
-
-    def send_both(source, target, slot):
-        return [send(source, target.at[which], which, slot) for which in (1, 0)]
-
-    x0_copies = send_both(x0_ref, x0_in, 0)
+
+    def send_rows(source, target, slot, rows, other=None):
+        by_col = describe(source.at[rows], target.at[1, rows], 1, slot)
+        by_row = describe(source.at[rows], target.at[0, rows], 0, slot)
+        if other is None:
+            by_col.start()
+        else:
+            @elsewhere
+            def _():
+                by_col.start()
+
+            @on_last
+            def _():
+                describe(other.at[rows], target.at[1, rows], 1, slot).start()
+
+        by_row.start()
+        return [by_col, by_row]
+
+    whole = pl.ds(0, width)
+    x0_copies = send_rows(x0_ref, x0_in, 0, whole)
 
     loads = []
     for slot, (source, target) in enumerate(
@@ -119,7 +155,29 @@
 
     by_rows(0, width, first_round)
     gradient(0, g0)
-    g0_copies = send_both(g0, g0_in, 1)
+    g0_col = describe(g0, g0_in.at[1], 1, 1)
+    g0_row = describe(g0, g0_in.at[0], 0, 1)
+    g0_row.start()
+
+    far_copies = []
+    for part in range(PIECES):
+        rows = pl.ds(part * piece, piece)
+        far_copies.append(
+            pltpu.make_async_remote_copy(
+                src_ref=g0.at[rows], dst_ref=far_in.at[rows],
+                send_sem=far_send.at[part], recv_sem=far_recv.at[part],
+                device_id={"col": 1}, device_id_type=MESH,
+            )
+        )
+
+    @elsewhere
+    def _():
+        g0_col.start()
+
+    @on_last
+    def _():
+        for copy in far_copies[:EARLY]:
+            copy.start()
 
     for copy in x0_copies:
         copy.wait()
@@ -130,21 +188,57 @@
         xb[rows, :] = moved.astype(bf16)
 
     by_rows(0, width, first_move)
-    x1_copies = send_both(x1, x1_in, 2)
+
+    @on_last
+    def _():
+        def make_mix2(rows):
+            mix2[rows, :] = x1[rows, :] - step_rate * g0[rows, :]
+
+        by_rows(0, width, make_mix2)
+
+    x1_copies = send_rows(x1, x1_in, 2, whole, mix2)
     gradient(1, g1)
-    for copy in g0_copies:
-        copy.wait()
-
-    def first_track(rows):
-        y1[rows, :] = mixed(g0, g0_in, rows) + g1[rows, :] - g0[rows, :]
-
-    by_rows(0, width, first_track)
-    y1_copies = []
-    for part in range(PIECES):
-        rows = pl.ds(part * piece, piece)
-        y1_copies.append(
-            [send(y1.at[rows], y1_in.at[which, rows], which, 3 + part) for which in (1, 0)]
-        )
+    g0_row.wait()
+    on_first, beyond = where(first)
+
+    @on_first
+    def _():
+        def first_track(rows):
+            y1[rows, :] = (
+                w[0] * g0[rows, :] + w[1] * g0_in[0, rows, :] + g1[rows, :] - g0[rows, :]
+            )
+
+        by_rows(0, width, first_track)
+
+    @beyond
+    def _():
+        g0_col.wait_recv()
+
+        def first_track(rows):
+            y1[rows, :] = mixed(g0, g0_in, rows) + g1[rows, :] - g0[rows, :]
+
+        by_rows(0, width, first_track)
+
+    @on_last
+    def _():
+        def make_mix3(rows):
+            mix3[rows, :] = y1[rows, :] + w[0] * g0[rows, :] + w[1] * g0_in[0, rows, :]
+
+        by_rows(0, width, make_mix3)
+
+    y1_copies = [
+        send_rows(y1, y1_in, 3 + part, pl.ds(part * piece, piece), mix3)
+        for part in range(PIECES)
+    ]
+
+    @elsewhere
+    def _():
+        g0_col.wait_send()
+
+    @on_last
+    def _():
+        for copy in far_copies[EARLY:]:
+            copy.start()
 
     for copy in x1_copies:
         copy.wait()
@@ -160,21 +254,39 @@
     def second_track(rows):
         outy_ref[rows, :] = mixed(y1, y1_in, rows) + g2[rows, :] - g1[rows, :]
 
+    def second_track_far(rows):
+        second = w[2] * (y1_in[1, rows, :] + w[2] * far_in[rows, :])
+        outy_ref[rows, :] = (
+            w[0] * y1[rows, :] + w[1] * y1_in[0, rows, :] + second
+            + g2[rows, :] - g1[rows, :]
+        )
+
+    on_second, others = where(second)
     for part in range(PIECES):
         for copy in y1_copies[part]:
             copy.wait()
-        by_rows(part * piece, (part + 1) * piece, second_track)
+
+        @on_second
+        def _(part=part):
+            far_copies[part].wait_recv()
+            by_rows(part * piece, (part + 1) * piece, second_track_far)
+
+        @others
+        def _(part=part):
+            by_rows(part * piece, (part + 1) * piece, second_track)
+
+    @on_last
+    def _():
+        for copy in far_copies:
+            copy.wait_send()
 
 
 def write_out(x_ref, y_ref, x_hbm, y_hbm, sems):
-    rows = x_ref.shape[0] // OUT_PIECES
     copies = []
-    for part in range(OUT_PIECES):
-        here = pl.ds(part * rows, rows)
-        for which, (source, target) in enumerate(((x_ref, x_hbm), (y_ref, y_hbm))):
-            copy = pltpu.make_async_copy(source.at[here], target.at[here], sems.at[which, part])
-            copy.start()
-            copies.append(copy)
+    for slot, (source, target) in enumerate(((x_ref, x_hbm), (y_ref, y_hbm))):
+        copy = pltpu.make_async_copy(source, target, sems.at[slot])
+        copy.start()
+        copies.append(copy)
     for copy in copies:
         copy.wait()
 
@@ -205,9 +317,12 @@
                 pltpu.VMEM((width, features), jnp.bfloat16),
                 pltpu.VMEM((pool, features), jnp.bfloat16),
                 arrivals, arrivals, arrivals, arrivals,
+                field, field, field,
                 pltpu.SemaphoreType.DMA((6,)),
                 pltpu.SemaphoreType.DMA((2, 3 + PIECES)),
                 pltpu.SemaphoreType.DMA((2, 3 + PIECES)),
+                pltpu.SemaphoreType.DMA((PIECES,)),
+                pltpu.SemaphoreType.DMA((PIECES,)),
             ],
             compiler_params=pltpu.CompilerParams(
                 collective_id=0, has_side_effects=True, vmem_limit_bytes=54_000_000
@@ -225,7 +340,7 @@
             out_shape=(shape, shape),
             in_specs=[pl.BlockSpec(memory_space=pltpu.VMEM)] * 2,
             out_specs=(in_hbm,) * 2,
-            scratch_shapes=[pltpu.SemaphoreType.DMA((2, OUT_PIECES))],
+            scratch_shapes=[pltpu.SemaphoreType.DMA((2,))],
             compiler_params=pltpu.CompilerParams(vmem_limit_bytes=2**20),
         )(final_proj, final_tracker)
         return final_proj[None, None], final_tracker[None, None]

time: 189 us -> 188 us (level)
  Pallas kernels: 188 us -> 186 us
    pallas_call x1, Pallas kernels: 186 us -> 184 us  [on_device(): pl.pallas_call(functools.partial(kernel, sizes), out_shape=(pltpu.VMEM((w...]
where the time goes in v4:
time: 188 us; the launch traced here: 187 us
  Pallas kernels  186 us (99%)
    pallas_call x1, Pallas kernels, on_device(): pl.pallas_call(functools.partial(kernel, sizes), out_shape=(pltpu.VMEM((w...  184 us

profile of v4, /device:TPU:0, one launch (start us, length us, event | category | flops | bytes accessed | tf_op | source)
XLA Modules:
  0.0 186.8 jit_solution(17409472477499946563)
XLA Ops:
  0.6 184.2 %shard_map.77 = (f32[1024,512]{1,0:T(8,128)S(1)}, f32[1024,512]{1,0:T(8,128)S(1)}) custom-call(f32[1024,512]{1,0:T(8,128)} %bitcast.8, bf16[1536,1024]{1,0:T(8,128)(2,1)} %bitcast.6, bf16[1536,1024]{1,0:T(8,128)(2,1)} %bitcast.7, s32[3,1,1536]{2,1,0:T(1,128)} %bitcast.9, bf16[512,1024]{1,0:T(8,128)(2,1)} %fo_hbm.1, s32[3]{0:T(128)} %num_hbm.1), custom_call_target="tpu_custom_call" | custom-call | tf_op jit(solution)/shard_map/pallas_call | solution.py:305
  184.8 2.0 %shard_map.78 = (f32[1024,512]{1,0:T(8,128)}, f32[1024,512]{1,0:T(8,128)}) custom-call(f32[1024,512]{1,0:T(8,128)S(1)} %get-tuple-element.6.x_ref, f32[1024,512]{1,0:T(8,128)S(1)} %get-tuple-element.7.y_ref), custom_call_target="tpu_custom_call" | custom-call | tf_op jit(solution)/shard_map/pallas_call | solution.py:338

commit v5 on v4

--- a/solution.py
+++ b/solution.py
@@ -18,7 +18,7 @@
 def kernel(sizes, x0_ref, tok_hbm, tgt_hbm, ids_hbm, fo_hbm, num_hbm, outx_ref, outy_ref,
            tok, tgt, ids, fo, num_ref, x0, x1, g0, g1, g2, y1, xb, bp,
            x0_in, g0_in, x1_in, y1_in, far_in, mix2, mix3,
-           local_sem, send_sem, recv_sem, far_send, far_recv):
+           local_sem, send_sem, recv_sem, far_send, far_recv, row_ready):
     pool, width = tok.shape
     features = x0.shape[1]
     factor = width ** (-0.5)
@@ -37,10 +37,8 @@
         return pl.when(condition), pl.when(jnp.logical_not(condition))
 
     barrier = pltpu.get_barrier_semaphore()
-    for axis in AXES:
-        pl.semaphore_signal(
-            barrier, inc=1, device_id={axis: left[axis]}, device_id_type=MESH
-        )
+    for there in ({"col": left["col"]}, {"row": right["row"]}):
+        pl.semaphore_signal(barrier, inc=1, device_id=there, device_id_type=MESH)
 
     @pl.when(second)
     def _():
@@ -86,7 +84,11 @@
         return [by_col, by_row]
 
     whole = pl.ds(0, width)
-    x0_copies = send_rows(x0_ref, x0_in, 0, whole)
+    x0_copies = [describe(x0_ref, x0_in.at[which], which, 0) for which in (1, 0)]
+    x0_copies[0].start()
+    pl.semaphore_signal(row_ready, inc=1, device_id={"row": left["row"]}, device_id_type=MESH)
+    pl.semaphore_wait(row_ready, 1)
+    x0_copies[1].start()
 
     loads = []
     for slot, (source, target) in enumerate(
@@ -323,6 +325,7 @@
                 pltpu.SemaphoreType.DMA((2, 3 + PIECES)),
                 pltpu.SemaphoreType.DMA((PIECES,)),
                 pltpu.SemaphoreType.DMA((PIECES,)),
+                pltpu.SemaphoreType.REGULAR,
             ],
             compiler_params=pltpu.CompilerParams(
                 collective_id=0, has_side_effects=True, vmem_limit_bytes=54_000_000

time: 188 us -> 187 us (level)
  no operation moved by 1% of the time
where the time goes in v5:
time: 187 us; the launch traced here: 186 us
  Pallas kernels  186 us (99%)
    pallas_call x1, Pallas kernels, on_device(): pl.pallas_call(functools.partial(kernel, sizes), out_shape=(pltpu.VMEM((w...  184 us

profile of v5, /device:TPU:0, one launch (start us, length us, event | category | flops | bytes accessed | tf_op | source)
XLA Modules:
  0.0 186.4 jit_solution(18331843663937954133)
XLA Ops:
  0.6 183.7 %shard_map.77 = (f32[1024,512]{1,0:T(8,128)S(1)}, f32[1024,512]{1,0:T(8,128)S(1)}) custom-call(f32[1024,512]{1,0:T(8,128)} %bitcast.8, bf16[1536,1024]{1,0:T(8,128)(2,1)} %bitcast.6, bf16[1536,1024]{1,0:T(8,128)(2,1)} %bitcast.7, s32[3,1,1536]{2,1,0:T(1,128)} %bitcast.9, bf16[512,1024]{1,0:T(8,128)(2,1)} %fo_hbm.1, s32[3]{0:T(128)} %num_hbm.1), custom_call_target="tpu_custom_call" | custom-call | tf_op jit(solution)/shard_map/pallas_call | solution.py:307
  184.3 2.0 %shard_map.78 = (f32[1024,512]{1,0:T(8,128)}, f32[1024,512]{1,0:T(8,128)}) custom-call(f32[1024,512]{1,0:T(8,128)S(1)} %get-tuple-element.6.x_ref, f32[1024,512]{1,0:T(8,128)S(1)} %get-tuple-element.7.y_ref), custom_call_target="tpu_custom_call" | custom-call | tf_op jit(solution)/shard_map/pallas_call | solution.py:341

commit v6 on v5

--- a/solution.py
+++ b/solution.py
@@ -10,8 +10,7 @@
 
 MESH = pl.DeviceIdType.MESH
 step_rate = 0.2
-PIECES = 8
-EARLY = 3
+TAIL = 64
 AXES = ("row", "col")
 
 
@@ -23,7 +22,7 @@
     features = x0.shape[1]
     factor = width ** (-0.5)
     f32, bf16 = jnp.float32, jnp.bfloat16
-    piece = width // PIECES
+    early, bulk = 3 * width // 8, width - min(TAIL, width // 8)
     right, left = {}, {}
     for axis, n in zip(AXES, sizes):
         me = lax.axis_index(axis)
@@ -162,8 +161,8 @@
     g0_row.start()
 
     far_copies = []
-    for part in range(PIECES):
-        rows = pl.ds(part * piece, piece)
+    for part, (start, stop) in enumerate(((0, early), (early, bulk), (bulk, width))):
+        rows = pl.ds(start, stop - start)
         far_copies.append(
             pltpu.make_async_remote_copy(
                 src_ref=g0.at[rows], dst_ref=far_in.at[rows],
@@ -178,8 +177,7 @@
 
     @on_last
     def _():
-        for copy in far_copies[:EARLY]:
-            copy.start()
+        far_copies[0].start()
 
     for copy in x0_copies:
         copy.wait()
@@ -228,10 +226,23 @@
 
         by_rows(0, width, make_mix3)
 
-    y1_copies = [
-        send_rows(y1, y1_in, 3 + part, pl.ds(part * piece, piece), mix3)
-        for part in range(PIECES)
-    ]
+    parts = ((0, bulk), (bulk, width))
+    y1_copies = []
+    for part, (start, stop) in enumerate(parts):
+        rows = pl.ds(start, stop - start)
+        by_col = describe(y1.at[rows], y1_in.at[1, rows], 1, 3 + part)
+
+        @elsewhere
+        def _(by_col=by_col):
+            by_col.start()
+
+        @on_last
+        def _(rows=rows, part=part):
+            describe(mix3.at[rows], y1_in.at[1, rows], 1, 3 + part).start()
+
+        y1_copies.append([by_col])
+    y1_row = describe(y1, y1_in.at[0], 0, 3)
+    y1_row.start()
 
     @elsewhere
     def _():
@@ -239,7 +250,7 @@
 
     @on_last
     def _():
-        for copy in far_copies[EARLY:]:
+        for copy in far_copies[1:]:
             copy.start()
 
     for copy in x1_copies:
@@ -263,19 +274,21 @@
             + g2[rows, :] - g1[rows, :]
         )
 
+    y1_row.wait()
     on_second, others = where(second)
-    for part in range(PIECES):
+    for part, (start, stop) in enumerate(parts):
         for copy in y1_copies[part]:
             copy.wait()
 
         @on_second
-        def _(part=part):
-            far_copies[part].wait_recv()
-            by_rows(part * piece, (part + 1) * piece, second_track_far)
+        def _(part=part, start=start, stop=stop):
+            for copy in (far_copies[:2], far_copies[2:])[part]:
+                copy.wait_recv()
+            by_rows(start, stop, second_track_far)
 
         @others
-        def _(part=part):
-            by_rows(part * piece, (part + 1) * piece, second_track)
+        def _(start=start, stop=stop):
+            by_rows(start, stop, second_track)
 
     @on_last
     def _():
@@ -321,10 +334,10 @@
                 arrivals, arrivals, arrivals, arrivals,
                 field, field, field,
                 pltpu.SemaphoreType.DMA((6,)),
-                pltpu.SemaphoreType.DMA((2, 3 + PIECES)),
-                pltpu.SemaphoreType.DMA((2, 3 + PIECES)),
-                pltpu.SemaphoreType.DMA((PIECES,)),
-                pltpu.SemaphoreType.DMA((PIECES,)),
+                pltpu.SemaphoreType.DMA((2, 5)),
+                pltpu.SemaphoreType.DMA((2, 5)),
+                pltpu.SemaphoreType.DMA((3,)),
+                pltpu.SemaphoreType.DMA((3,)),
                 pltpu.SemaphoreType.REGULAR,
             ],
             compiler_params=pltpu.CompilerParams(

time: 187 us -> 187 us (level)
  no operation moved by 1% of the time
where the time goes in v6:
time: 187 us; the launch traced here: 186 us
  Pallas kernels  185 us (99%)
    pallas_call x1, Pallas kernels, on_device(): pl.pallas_call(functools.partial(kernel, sizes), out_shape=(pltpu.VMEM((w...  183 us

profile of v6, /device:TPU:0, one launch (start us, length us, event | category | flops | bytes accessed | tf_op | source)
XLA Modules:
  0.0 186.0 jit_solution(12555633490733538690)
XLA Ops:
  0.6 183.3 %shard_map.77 = (f32[1024,512]{1,0:T(8,128)S(1)}, f32[1024,512]{1,0:T(8,128)S(1)}) custom-call(f32[1024,512]{1,0:T(8,128)} %bitcast.8, bf16[1536,1024]{1,0:T(8,128)(2,1)} %bitcast.6, bf16[1536,1024]{1,0:T(8,128)(2,1)} %bitcast.7, s32[3,1,1536]{2,1,0:T(1,128)} %bitcast.9, bf16[512,1024]{1,0:T(8,128)(2,1)} %fo_hbm.1, s32[3]{0:T(128)} %num_hbm.1), custom_call_target="tpu_custom_call" | custom-call | tf_op jit(solution)/shard_map/pallas_call | solution.py:320
  184.0 2.0 %shard_map.78 = (f32[1024,512]{1,0:T(8,128)}, f32[1024,512]{1,0:T(8,128)}) custom-call(f32[1024,512]{1,0:T(8,128)S(1)} %get-tuple-element.6.x_ref, f32[1024,512]{1,0:T(8,128)S(1)} %get-tuple-element.7.y_ref), custom_call_target="tpu_custom_call" | custom-call | tf_op jit(solution)/shard_map/pallas_call | solution.py:354

commit v7 on v6

--- a/solution.py
+++ b/solution.py
@@ -36,14 +36,14 @@
         return pl.when(condition), pl.when(jnp.logical_not(condition))
 
     barrier = pltpu.get_barrier_semaphore()
+    @pl.when(second)
+    def _():
+        pl.semaphore_signal(
+            barrier, inc=1, device_id={"col": n_col - 1}, device_id_type=MESH
+        )
+
     for there in ({"col": left["col"]}, {"row": right["row"]}):
         pl.semaphore_signal(barrier, inc=1, device_id=there, device_id_type=MESH)
-
-    @pl.when(second)
-    def _():
-        pl.semaphore_signal(
-            barrier, inc=1, device_id={"col": n_col - 1}, device_id_type=MESH
-        )
 
     on_last, elsewhere = where(last)
 

time: 187 us -> 187 us (level)
  no operation moved by 1% of the time
where the time goes in v7:
time: 187 us; the launch traced here: 186 us
  Pallas kernels  185 us (99%)
    pallas_call x1, Pallas kernels, on_device(): pl.pallas_call(functools.partial(kernel, sizes), out_shape=(pltpu.VMEM((w...  183 us

profile of v7, /device:TPU:0, one launch (start us, length us, event | category | flops | bytes accessed | tf_op | source)
XLA Modules:
  0.0 186.0 jit_solution(12826121402968064499)
XLA Ops:
  0.6 183.4 %shard_map.77 = (f32[1024,512]{1,0:T(8,128)S(1)}, f32[1024,512]{1,0:T(8,128)S(1)}) custom-call(f32[1024,512]{1,0:T(8,128)} %bitcast.8, bf16[1536,1024]{1,0:T(8,128)(2,1)} %bitcast.6, bf16[1536,1024]{1,0:T(8,128)(2,1)} %bitcast.7, s32[3,1,1536]{2,1,0:T(1,128)} %bitcast.9, bf16[512,1024]{1,0:T(8,128)(2,1)} %fo_hbm.1, s32[3]{0:T(128)} %num_hbm.1), custom_call_target="tpu_custom_call" | custom-call | tf_op jit(solution)/shard_map/pallas_call | solution.py:320
  184.0 2.0 %shard_map.78 = (f32[1024,512]{1,0:T(8,128)}, f32[1024,512]{1,0:T(8,128)}) custom-call(f32[1024,512]{1,0:T(8,128)S(1)} %get-tuple-element.6.x_ref, f32[1024,512]{1,0:T(8,128)S(1)} %get-tuple-element.7.y_ref), custom_call_target="tpu_custom_call" | custom-call | tf_op jit(solution)/shard_map/pallas_call | solution.py:354
